TPU v7x, 32 devices: a whole 2x2x4 slice. The times are simulated.
32 devices in a mesh: row: 4 (over y, core), col: 8 (over z, x).
Axes of the slice: x: 2, y: 2, z: 4, core: 2. Of those that a mesh axis runs over, the one named last changes fastest.
Arguments:
- offsets: float32 [3, 8192], P(None, ('row', 'col')), may hold values from 0 to 11
- cells: int32 [3, 64], replicated, may hold values from 0 to 3, as said below
- types: int32 [8192], P(('row', 'col')), may hold values from 0 to 3, as said below
- mask: int32 [4, 16, 4, 16], P(None, 'col', 'row'), may hold values from 0 to 1, as said below
- chi_table: float32 [4], replicated, may hold values from 2 to 10.1
- eta_table: float32 [4], replicated, may hold values from 13 to 18
- gamma_table: float32 [4], replicated, may hold values from 0.4 to 0.8
Outputs:
- charges: float32 [8192], P(('row', 'col'))
Inputs may be any that keep to these rules, and one draw needn't show every extreme that they name: The cells of the blocks are a permutation of all 4 x 4 x 4 cells: each cell holds exactly one block. The mask marks a pair of blocks exactly when their cells are equal or adjacent on the periodic grid in every dimension; it is symmetric and each block is marked with exactly 27 blocks, itself included. `types`: types 2 and 3 grow more common along the atoms, from none in the first 256 atoms to nearly all in the last.
All inputs are finite; a program needn't handle non-finite values.
Results may differ from a plain program's by a relative error of at most 0.0003.
Values sent between devices are 32-bit elements; how exact they have to be, the bound alone decides.
No kernel may reach another device: no remote copies, remote signals or barrier semaphores. Data moves between devices by JAX's collectives and lax.ppermute only.
A program may use at most 64 MiB of HBM per device.

v0:
```python
import jax
import jax.numpy as jnp
from jax import lax
from jax.sharding import PartitionSpec as P

BLOCK = 128
GRID_Z = 4
ITERS = 3
coulomb = 14.4
cutoff = 10.0
cell_side = 11.0
pair_group = 64


def taper(dist):
    xval = dist / cutoff
    poly = 1.0 + xval**4 * (-35.0 + xval * (84.0 + xval * (-70.0 + 20.0 * xval)))
    return jnp.where(xval < 1.0, poly, 0.0)


def coupling(tgt, src, tgt_cell, src_cell, same, grid):
    half = grid[:, None] // 2
    shift = ((src_cell - tgt_cell + half) % grid[:, None] - half).astype(jnp.float32) * cell_side
    radius_sq = jnp.zeros((tgt.shape[1], tgt.shape[2], src.shape[2]), jnp.float32)
    for comp in range(3):
        delta = shift[comp][:, None, None] + src[comp][:, None, :] - tgt[comp][:, :, None]
        radius_sq = radius_sq + delta * delta
    dist = jnp.sqrt(radius_sq)
    paired = tgt[3][:, :, None] * src[3][:, None, :]
    shield = 1.0 / (paired * jnp.sqrt(paired))
    kern = coulomb * taper(dist) / jnp.cbrt(radius_sq * dist + shield)
    width = tgt.shape[2]
    diag = jnp.arange(width)[:, None] == jnp.arange(width)[None, :]
    return jnp.where(same[:, None, None] & diag[None], 0.0, kern)


def pick(kinds, table):
    return jnp.sum(jnp.where(kinds, table[:, None], 0.0), axis=0)


def paired_sums(residual, image):
    return lax.psum(
        (jnp.sum(residual * residual, axis=1), jnp.sum(residual * image, axis=1)), ("row", "col")
    )


def per_device(offsets, cells, types, mask, chi_table, eta_table, gamma_table):
    n_row = lax.axis_size("row")
    n_col = lax.axis_size("col")
    row_at = lax.axis_index("row")
    col_at = lax.axis_index("col")
    span = types.shape[0]
    bpd = span // BLOCK
    n_tgt = n_row * bpd
    n_src = n_col * bpd
    grid = jnp.array([n_row, n_src // GRID_Z, GRID_Z], jnp.int32)
    kinds = jnp.arange(chi_table.shape[0])[:, None] == types[None, :]
    chi = pick(kinds, chi_table)
    eta = pick(kinds, eta_table)
    gamma = pick(kinds, gamma_table)
    geo = jnp.concatenate([offsets, gamma[None]], axis=0)
    src_geo = lax.all_gather(geo, "col", axis=1, tiled=True).reshape(4, n_src, BLOCK)
    tgt_geo = lax.all_gather(geo, "row", axis=1, tiled=True).reshape(4, n_tgt, BLOCK)
    tgt_ids = (
        (jnp.arange(n_row, dtype=jnp.int32)[:, None] * n_col + col_at) * bpd
        + jnp.arange(bpd, dtype=jnp.int32)[None, :]
    ).reshape(n_tgt)
    src_ids = row_at * n_src + jnp.arange(n_src, dtype=jnp.int32)
    tgt_cells = jnp.take(cells, tgt_ids, axis=1)
    src_cells = jnp.take(cells, src_ids, axis=1)
    tile = mask.reshape(n_tgt * n_src)
    count = jnp.sum(tile)
    slots = jnp.nonzero(tile, size=n_tgt * n_src + pair_group, fill_value=0)[0].astype(jnp.int32)
    groups = (count + pair_group - 1) // pair_group
    tgt_range = jnp.arange(n_tgt, dtype=jnp.int32)

    def block_kernel(step):
        picked = lax.dynamic_slice_in_dim(slots, step * pair_group, pair_group)
        live = step * pair_group + jnp.arange(pair_group) < count
        tgt_blk = picked // n_src
        src_blk = picked % n_src
        kern = coupling(
            tgt_geo[:, tgt_blk],
            src_geo[:, src_blk],
            tgt_cells[:, tgt_blk],
            src_cells[:, src_blk],
            tgt_ids[tgt_blk] == src_ids[src_blk],
            grid,
        )
        return (jnp.where(live[:, None, None], kern, 0.0), tgt_blk, src_blk)

    def apply(direction):
        remote = lax.all_gather(direction, "col", axis=1, tiled=True).reshape(2, n_src, BLOCK)

        def turn(step, acc):
            kern, tgt_blk, src_blk = block_kernel(step)
            contrib = jnp.einsum(
                "gij,kgj->kgi", kern, remote[:, src_blk], precision=lax.Precision.HIGHEST
            )
            owners = (tgt_range[:, None] == tgt_blk[None, :]).astype(jnp.float32)
            return acc + jnp.einsum("tg,kgi->kti", owners, contrib, precision=lax.Precision.HIGHEST)

        acc = lax.fori_loop(0, groups, turn, jnp.zeros((2, n_tgt, BLOCK), jnp.float32))
        summed = lax.psum_scatter(
            acc.reshape(2, n_tgt * BLOCK), "row", scatter_dimension=1, tiled=True
        )
        return summed + eta[None] * direction

    rhs = jnp.stack([-chi, -jnp.ones_like(chi)], axis=0)
    solution = jnp.zeros_like(rhs)
    residual = rhs
    image = apply(residual)
    norm_now, product = paired_sums(residual, image)
    alpha = norm_now / product
    direction = residual
    along = image
    for step in range(ITERS):
        solution = solution + alpha[:, None] * direction
        residual = residual - alpha[:, None] * along
        if step + 1 < ITERS:
            image = apply(residual)
            norm_next, product = paired_sums(residual, image)
            ratio = norm_next / norm_now
            alpha = norm_next / (product - ratio * norm_next / alpha)
            direction = residual + ratio[:, None] * direction
            along = image + ratio[:, None] * along
            norm_now = norm_next
    totals = lax.psum(jnp.sum(solution, axis=1), ("row", "col"))
    return solution[0] - totals[0] / totals[1] * solution[1]


def solution(mesh):
    placed = (
        P(None, ("row", "col")),
        P(),
        P(("row", "col")),
        P(None, "col", "row", None),
        P(),
        P(),
        P(),
    )
    return jax.shard_map(
        per_device, mesh=mesh, in_specs=placed, out_specs=P(("row", "col")), check_vma=False
    )
```

profile of v0, /device:TPU:0, one launch (start us, length us, event | category | flops | bytes accessed | tf_op | source)
XLA Modules:
  0.0 517.9 jit_solution(5208578501713423526)
XLA Ops:
  6.5 1.4 fusion.200
  8.8 0.8 select_reduce_fusion
  10.3 32.4 %all_gather.16 = f32[4,2048]{1,0:T(4,128)S(1)} all-gather(f32[4,256]{1,0:T(4,128)S(1)} %pad_maximum_fusion), channel_id=1, replica_groups=mesh['row'=4,'col'=8] {'col'}, dimensions={1}, use_global_device_ids=true | all-gather | bytes 36864 | tf_op jit(solution)/shard_map/all_gather | solution.py:62
  42.7 5.2 %all_gather.17 = f32[4,1024]{1,0:T(4,128)S(1)} all-gather(f32[4,256]{1,0:T(4,128)S(1)} %pad_maximum_fusion), channel_id=1, replica_groups=mesh['row'=4,'col'=8] {'row'}, dimensions={1}, use_global_device_ids=true | all-gather | bytes 20480 | tf_op jit(solution)/shard_map/all_gather | solution.py:63
  49.1 1.4 scatter_custom_fusion
  52.3 26.1 %all_gather.15 = f32[2,2048]{1,0:T(2,128)S(1)} all-gather(f32[2,256]{1,0:T(2,128)S(1)} %stack.2), channel_id=1, replica_groups=mesh['row'=4,'col'=8] {'col'}, dimensions={1}, use_global_device_ids=true | all-gather | bytes 18432 | tf_op jit(solution)/shard_map/all_gather | solution.py:93
  79.2 28.1 %while.48 = (s32[]{:T(128)}, f32[2,8,128]{2,1,0:T(8,128)S(1)}, s32[]{:T(128)}, s32[192]{0:T(256)S(1)}, f32[2,16,128]{2,0,1:T(2,128)S(1)}, /*index=5*/s32[]{:T(12...) while((s32[]{:T(128)}, f32[2,8,128]{2,1,0:T(8,128)S(1)}, ...), condition=%wide.region_11.13_spmd.clone.clone.clone, body=%wide.region_10.12_spmd.sunk.clone.clone.clone.sunk | while | flops 59296340 | bytes 1905783 | solution.py:103
  79.3 0.8 gather_fusion.1
  80.8 5.6 %fusion.258 = (pred[64]{0:T(512)(128)(4,1)S(1)}, s32[64]{0:T(128)S(1)}, pred[64]{0:T(512)(128)(4,1)S(1)}) fusion(s32[64]{0:T(128)S(1)} %gather_fusion.1, s32[]{:T(128)} %bitcast.211, s32[]{:T(128)} %bitcast.212, s32[]{:T(128)} %bitcast.213, s32[]{:T(128)} %bitcast.214, s32[]{:T(128)} %bitcast.215, s32[]{:T(128)} %bitcast.216, s32[]{:T(128)} %bitcast.217, ...), kind=kLoop, calls=%fused_computation.109.clone.1 | loop fusion | flops 2048 | bytes 1196 | tf_op jit(solution)/shard_map/while/body/eq | solution.py:87
  90.3 16.9 %fusion.261 = f32[2,64,128]{2,0,1:T(2,128)S(1)} fusion(f32[64,128]{1,0:T(8,128)S(1)} %bitcast.296, f32[64,128]{1,0:T(8,128)S(1)} %bitcast.302, f32[64,128]{1,0:T(8,128)S(1)} %bitcast.300, f32[64,128]{1,0:T(8,128)S(1)} %broadcast_add_fusion.18, f32[64,128]{1,0:T(8,128)S(1)} %bitcast.301, f32[64,128]{1,0:T(8,128)S(1)} %broadcast_add_fusion.19, ...), kind=kOutput, calls=%fused_computation.71.clone.1 | convolution fusion | flops 57671680 | bytes 409728 | tf_op jit(solution)/shard_map/while/body/gij,kgj->kgi/dot_general | solution.py:97
  107.4 1.0 copy.39
  108.5 42.6 %reduce-scatter.10.cloned.1.call-done = f32[256,2]{1,0:T(8,128)} async-done(((f32[1024,2]{1,0:T(8,128)}), f32[256,2]{1,0:T(8,128)}) %reduce-scatter.10.cloned.1.call-update) | async-done | bytes 2064
  151.0 1.0 copy.34
  152.2 39.3 %all-reduce.4 = (f32[2]{0:T(128)S(1)}, f32[2]{0:T(128)S(1)}) all-reduce(f32[2]{0:T(128)S(1)} %get-tuple-element.1154, f32[2]{0:T(128)S(1)} %get-tuple-element.1153), channel_id=1, replica_groups=mesh['row'=4,'col'=8] {'row','col'}, use_global_device_ids=true, to_apply=%region_2.3 | all-reduce | flops 4 | bytes 32 | tf_op jit(solution)/shard_map/psum | solution.py:42
  191.6 26.1 %all_gather.18 = f32[2,2048]{1,0:T(2,128)S(1)} all-gather(f32[2,256]{1,0:T(2,128)S(1)} %multiply_subtract_fusion.1), channel_id=1, replica_groups=mesh['row'=4,'col'=8] {'col'}, dimensions={1}, use_global_device_ids=true | all-gather | bytes 18432 | tf_op jit(solution)/shard_map/all_gather | solution.py:93
  217.7 28.2 %while.49 = (s32[]{:T(128)}, f32[2,8,128]{2,1,0:T(8,128)S(1)}, s32[]{:T(128)}, s32[192]{0:T(256)S(1)}, f32[2,16,128]{2,0,1:T(2,128)S(1)}, /*index=5*/s32[]{:T(12...) while((s32[]{:T(128)}, f32[2,8,128]{2,1,0:T(8,128)S(1)}, ...), condition=%wide.region_19.21_spmd.clone.clone.clone, body=%wide.region_18.20_spmd.sunk.clone.clone.clone.sunk | while | flops 59296340 | bytes 1905783 | solution.py:103
  217.8 0.8 gather_fusion.7
  219.3 5.7 %fusion.269 = (pred[64]{0:T(512)(128)(4,1)S(1)}, s32[64]{0:T(128)S(1)}, pred[64]{0:T(512)(128)(4,1)S(1)}) fusion(s32[64]{0:T(128)S(1)} %gather_fusion.7, s32[]{:T(128)} %bitcast.234, s32[]{:T(128)} %bitcast.235, s32[]{:T(128)} %bitcast.236, s32[]{:T(128)} %bitcast.237, s32[]{:T(128)} %bitcast.238, s32[]{:T(128)} %bitcast.239, s32[]{:T(128)} %bitcast.240, ...), kind=kLoop, calls=%fused_computation.202.clone.1 | loop fusion | flops 2048 | bytes 1196 | tf_op jit(solution)/shard_map/while/body/eq | solution.py:87
  228.8 16.9 %fusion.272 = f32[2,64,128]{2,0,1:T(2,128)S(1)} fusion(f32[64,128]{1,0:T(8,128)S(1)} %bitcast.297, f32[64,128]{1,0:T(8,128)S(1)} %bitcast.306, f32[64,128]{1,0:T(8,128)S(1)} %bitcast.304, f32[64,128]{1,0:T(8,128)S(1)} %broadcast_add_fusion.21, f32[64,128]{1,0:T(8,128)S(1)} %bitcast.305, f32[64,128]{1,0:T(8,128)S(1)} %broadcast_add_fusion.22, ...), kind=kOutput, calls=%fused_computation.164.clone.1 | convolution fusion | flops 57671680 | bytes 409728 | tf_op jit(solution)/shard_map/while/body/gij,kgj->kgi/dot_general | solution.py:97
  245.9 1.0 copy.40
  247.0 42.1 %reduce-scatter.12.cloned.1.call-done = f32[256,2]{1,0:T(8,128)} async-done(((f32[1024,2]{1,0:T(8,128)}), f32[256,2]{1,0:T(8,128)}) %reduce-scatter.12.cloned.1.call-update) | async-done | bytes 2064
  289.1 1.0 copy.36
  290.3 39.3 %all-reduce.3 = (f32[2]{0:T(128)S(1)}, f32[2]{0:T(128)S(1)}) all-reduce(f32[2]{0:T(128)S(1)} %get-tuple-element.1152, f32[2]{0:T(128)S(1)} %get-tuple-element.1151), channel_id=1, replica_groups=mesh['row'=4,'col'=8] {'row','col'}, use_global_device_ids=true, to_apply=%region_17.19 | all-reduce | flops 4 | bytes 32 | tf_op jit(solution)/shard_map/psum | solution.py:42
  329.7 26.1 %all_gather.19 = f32[2,2048]{1,0:T(2,128)S(1)} all-gather(f32[2,256]{1,0:T(2,128)S(1)} %multiply_subtract_fusion), channel_id=1, replica_groups=mesh['row'=4,'col'=8] {'col'}, dimensions={1}, use_global_device_ids=true | all-gather | bytes 18432 | tf_op jit(solution)/shard_map/all_gather | solution.py:93
  355.8 28.2 %while.50 = (s32[]{:T(128)}, f32[2,8,128]{2,1,0:T(8,128)S(1)}, s32[]{:T(128)}, s32[192]{0:T(256)S(1)}, f32[2,16,128]{2,0,1:T(2,128)S(1)}, /*index=5*/s32[]{:T(12...) while((s32[]{:T(128)}, f32[2,8,128]{2,1,0:T(8,128)S(1)}, ...), condition=%wide.region_26.28_spmd.clone.clone.clone, body=%wide.region_25.27_spmd.sunk.clone.clone.clone.sunk | while | flops 59296340 | bytes 1905783 | solution.py:103
  357.4 5.7 %fusion.280 = (pred[64]{0:T(512)(128)(4,1)S(1)}, s32[64]{0:T(128)S(1)}, pred[64]{0:T(512)(128)(4,1)S(1)}) fusion(s32[64]{0:T(128)S(1)} %gather_fusion.13, s32[]{:T(128)} %bitcast.257, s32[]{:T(128)} %bitcast.258, s32[]{:T(128)} %bitcast.259, s32[]{:T(128)} %bitcast.260, s32[]{:T(128)} %bitcast.261, s32[]{:T(128)} %bitcast.262, s32[]{:T(128)} %bitcast.263, ...), kind=kLoop, calls=%fused_computation.295.clone.1 | loop fusion | flops 2048 | bytes 1196 | tf_op jit(solution)/shard_map/while/body/eq | solution.py:87
  366.9 16.9 %fusion.283 = f32[2,64,128]{2,0,1:T(2,128)S(1)} fusion(f32[64,128]{1,0:T(8,128)S(1)} %bitcast.298, f32[64,128]{1,0:T(8,128)S(1)} %bitcast.310, f32[64,128]{1,0:T(8,128)S(1)} %bitcast.308, f32[64,128]{1,0:T(8,128)S(1)} %broadcast_add_fusion.24, f32[64,128]{1,0:T(8,128)S(1)} %bitcast.309, f32[64,128]{1,0:T(8,128)S(1)} %broadcast_add_fusion.25, ...), kind=kOutput, calls=%fused_computation.257.clone.1 | convolution fusion | flops 57671680 | bytes 409728 | tf_op jit(solution)/shard_map/while/body/gij,kgj->kgi/dot_general | solution.py:97
  384.0 1.0 copy.41
  385.1 42.1 %reduce-scatter.14.cloned.1.call-done = f32[256,2]{1,0:T(8,128)} async-done(((f32[1024,2]{1,0:T(8,128)}), f32[256,2]{1,0:T(8,128)}) %reduce-scatter.14.cloned.1.call-update) | async-done | bytes 2064
  427.2 1.0 copy.38
  428.3 39.3 %all-reduce.2 = (f32[2]{0:T(128)S(1)}, f32[2]{0:T(128)S(1)}) all-reduce(f32[2]{0:T(128)S(1)} %get-tuple-element.1150, f32[2]{0:T(128)S(1)} %get-tuple-element.1149), channel_id=1, replica_groups=mesh['row'=4,'col'=8] {'row','col'}, use_global_device_ids=true, to_apply=%region_24.26 | all-reduce | flops 4 | bytes 32 | tf_op jit(solution)/shard_map/psum | solution.py:42
  467.8 41.0 %psum.55 = f32[2]{0:T(128)S(1)} all-reduce(f32[2]{0:T(128)S(1)} %get-tuple-element.1248), channel_id=1, replica_groups=mesh['row'=4,'col'=8] {'row','col'}, use_global_device_ids=true, to_apply=%region_31.33 | all-reduce | flops 2 | bytes 16 | tf_op jit(solution)/shard_map/psum | solution.py:128
  (110 shorter events, 21.8 us)
Async XLA Ops:
  6.5 144.5 %reduce-scatter.10.cloned.1.call-start = ((), (), s32[]{:S(2)}) async-start(), calls=%async_computation.3 | async-start | bytes 655360
  108.4 180.7 %reduce-scatter.12.cloned.1.call-start = ((), (), s32[]{:S(2)}) async-start(), calls=%async_computation.4 | async-start | bytes 655360
  247.0 180.2 %reduce-scatter.14.cloned.1.call-start = ((), (), s32[]{:S(2)}) async-start(), calls=%async_computation.5 | async-start | bytes 655360
Sparse Core Ops, SparseCore 0:
  108.6 42.4 reduce-scatter.9
  247.1 41.9 reduce-scatter.11
  385.2 41.9 reduce-scatter.13
where the time goes:
time: 519 us; the launch traced here: 518 us
  blocking collectives  275 us (53%)
  waiting for transfers between devices  127 us (24%)
  matrix products  51.2 us (10%)
  other arithmetic  25.5 us (5%)
  local copies, waits for them, and re-layouts  24 us (5%)
  between operations  15.2 us (3%)
    unnamed x6, waiting for transfers between devices  127 us
    psum x3, blocking collectives, paired_sums(): lax.psum((jnp.sum(residual * residual, axis=1), jnp.sum(residual * image,...  118 us
    all_gather x3, blocking collectives, apply(): lax.all_gather(direction, 'col', axis=1, tiled=True)  78.3 us
    dot_general x3, matrix products, turn(): jnp.einsum('gij,kgj->kgi', kern, remote[:, src_blk], precision=lax.Precis...  50.8 us
    psum x1, blocking collectives, per_device(): totals = lax.psum(jnp.sum(solution, axis=1), ('row', 'col'))  41 us
    all_gather x1, blocking collectives, per_device(): lax.all_gather(geo, 'col', axis=1, tiled=True).reshape(4, n_src, BLOCK)  32.4 us
    eq x3, other arithmetic, block_kernel(): tgt_ids[tgt_blk] == src_ids[src_blk]  17 us
  transfers between devices with their start and end apart: 3, of which 3 were waited for; matrix products, arithmetic and copies ran while one was open for 0% of the time, Pallas kernels for 0%

commit v1 on v0

--- a/solution.py
+++ b/solution.py
@@ -10,6 +10,7 @@
 cutoff = 10.0
 cell_side = 11.0
 pair_group = 64
+loops_part = lambda obj: lax.psum(lax.psum(obj, axis_name="col"), axis_name="row")
 
 
 def taper(dist):
@@ -125,7 +126,7 @@
             direction = residual + ratio[:, None] * direction
             along = image + ratio[:, None] * along
             norm_now = norm_next
-    totals = lax.psum(jnp.sum(solution, axis=1), ("row", "col"))
+    totals = loops_part(jnp.sum(solution, axis=1))
     return solution[0] - totals[0] / totals[1] * solution[1]
 
 

time: 519 us -> 505 us (0.973)
  blocking collectives: 275 us -> 261 us
    psum x1 -> x2, blocking collectives: 41 us -> 26.7 us  [the longest x1 21.1 us: lax.psum(obj, axis_name='col')]
where the time goes in v1:
time: 505 us; the launch traced here: 504 us
  blocking collectives  261 us (52%)
  waiting for transfers between devices  127 us (25%)
  matrix products  51.2 us (10%)
  other arithmetic  25.5 us (5%)
  local copies, waits for them, and re-layouts  24 us (5%)
  between operations  15.2 us (3%)
    unnamed x6, waiting for transfers between devices  127 us
    psum x3, blocking collectives, paired_sums(): lax.psum((jnp.sum(residual * residual, axis=1), jnp.sum(residual * image,...  118 us
    all_gather x3, blocking collectives, apply(): lax.all_gather(direction, 'col', axis=1, tiled=True)  78.3 us
    dot_general x3, matrix products, turn(): jnp.einsum('gij,kgj->kgi', kern, remote[:, src_blk], precision=lax.Precis...  50.8 us
    all_gather x1, blocking collectives, per_device(): lax.all_gather(geo, 'col', axis=1, tiled=True).reshape(4, n_src, BLOCK)  32.4 us
    psum x1, blocking collectives, lax.psum(obj, axis_name='col')  21.1 us
    eq x3, other arithmetic, block_kernel(): tgt_ids[tgt_blk] == src_ids[src_blk]  17 us
  transfers between devices with their start and end apart: 3, of which 3 were waited for; matrix products, arithmetic and copies ran while one was open for 0% of the time, Pallas kernels for 0%

profile of v1, /device:TPU:0, one launch (start us, length us, event | category | flops | bytes accessed | tf_op | source)
XLA Modules:
  0.0 503.6 jit_solution(10917904094071344808)
XLA Ops:
  6.5 1.4 fusion.200
  8.8 0.8 select_reduce_fusion
  10.3 32.4 %all_gather.16 = f32[4,2048]{1,0:T(4,128)S(1)} all-gather(f32[4,256]{1,0:T(4,128)S(1)} %pad_maximum_fusion), channel_id=1, replica_groups=mesh['row'=4,'col'=8] {'col'}, dimensions={1}, use_global_device_ids=true | all-gather | bytes 36864 | tf_op jit(solution)/shard_map/all_gather | solution.py:63
  42.7 5.2 %all_gather.17 = f32[4,1024]{1,0:T(4,128)S(1)} all-gather(f32[4,256]{1,0:T(4,128)S(1)} %pad_maximum_fusion), channel_id=1, replica_groups=mesh['row'=4,'col'=8] {'row'}, dimensions={1}, use_global_device_ids=true | all-gather | bytes 20480 | tf_op jit(solution)/shard_map/all_gather | solution.py:64
  49.1 1.4 scatter_custom_fusion
  52.3 26.1 %all_gather.15 = f32[2,2048]{1,0:T(2,128)S(1)} all-gather(f32[2,256]{1,0:T(2,128)S(1)} %stack.2), channel_id=1, replica_groups=mesh['row'=4,'col'=8] {'col'}, dimensions={1}, use_global_device_ids=true | all-gather | bytes 18432 | tf_op jit(solution)/shard_map/all_gather | solution.py:94
  79.2 28.1 %while.48 = (s32[]{:T(128)}, f32[2,8,128]{2,1,0:T(8,128)S(1)}, s32[]{:T(128)}, s32[192]{0:T(256)S(1)}, f32[2,16,128]{2,0,1:T(2,128)S(1)}, /*index=5*/s32[]{:T(12...) while((s32[]{:T(128)}, f32[2,8,128]{2,1,0:T(8,128)S(1)}, ...), condition=%wide.region_11.13_spmd.clone.clone.clone, body=%wide.region_10.12_spmd.sunk.clone.clone.clone.sunk | while | flops 59296340 | bytes 1905783 | solution.py:104
  79.3 0.8 gather_fusion.1
  80.8 5.6 %fusion.258 = (pred[64]{0:T(512)(128)(4,1)S(1)}, s32[64]{0:T(128)S(1)}, pred[64]{0:T(512)(128)(4,1)S(1)}) fusion(s32[64]{0:T(128)S(1)} %gather_fusion.1, s32[]{:T(128)} %bitcast.211, s32[]{:T(128)} %bitcast.212, s32[]{:T(128)} %bitcast.213, s32[]{:T(128)} %bitcast.214, s32[]{:T(128)} %bitcast.215, s32[]{:T(128)} %bitcast.216, s32[]{:T(128)} %bitcast.217, ...), kind=kLoop, calls=%fused_computation.109.clone.1 | loop fusion | flops 2048 | bytes 1196 | tf_op jit(solution)/shard_map/while/body/eq | solution.py:88
  90.3 16.9 %fusion.261 = f32[2,64,128]{2,0,1:T(2,128)S(1)} fusion(f32[64,128]{1,0:T(8,128)S(1)} %bitcast.296, f32[64,128]{1,0:T(8,128)S(1)} %bitcast.302, f32[64,128]{1,0:T(8,128)S(1)} %bitcast.300, f32[64,128]{1,0:T(8,128)S(1)} %broadcast_add_fusion.18, f32[64,128]{1,0:T(8,128)S(1)} %bitcast.301, f32[64,128]{1,0:T(8,128)S(1)} %broadcast_add_fusion.19, ...), kind=kOutput, calls=%fused_computation.71.clone.1 | convolution fusion | flops 57671680 | bytes 409728 | tf_op jit(solution)/shard_map/while/body/gij,kgj->kgi/dot_general | solution.py:98
  107.4 1.0 copy.39
  108.5 42.6 %reduce-scatter.10.cloned.1.call-done = f32[256,2]{1,0:T(8,128)} async-done(((f32[1024,2]{1,0:T(8,128)}), f32[256,2]{1,0:T(8,128)}) %reduce-scatter.10.cloned.1.call-update) | async-done | bytes 2064
  151.0 1.0 copy.34
  152.2 39.3 %all-reduce.4 = (f32[2]{0:T(128)S(1)}, f32[2]{0:T(128)S(1)}) all-reduce(f32[2]{0:T(128)S(1)} %get-tuple-element.1154, f32[2]{0:T(128)S(1)} %get-tuple-element.1153), channel_id=1, replica_groups=mesh['row'=4,'col'=8] {'row','col'}, use_global_device_ids=true, to_apply=%region_2.3 | all-reduce | flops 4 | bytes 32 | tf_op jit(solution)/shard_map/psum | solution.py:43
  191.6 26.1 %all_gather.18 = f32[2,2048]{1,0:T(2,128)S(1)} all-gather(f32[2,256]{1,0:T(2,128)S(1)} %multiply_subtract_fusion.1), channel_id=1, replica_groups=mesh['row'=4,'col'=8] {'col'}, dimensions={1}, use_global_device_ids=true | all-gather | bytes 18432 | tf_op jit(solution)/shard_map/all_gather | solution.py:94
  217.7 28.2 %while.49 = (s32[]{:T(128)}, f32[2,8,128]{2,1,0:T(8,128)S(1)}, s32[]{:T(128)}, s32[192]{0:T(256)S(1)}, f32[2,16,128]{2,0,1:T(2,128)S(1)}, /*index=5*/s32[]{:T(12...) while((s32[]{:T(128)}, f32[2,8,128]{2,1,0:T(8,128)S(1)}, ...), condition=%wide.region_19.21_spmd.clone.clone.clone, body=%wide.region_18.20_spmd.sunk.clone.clone.clone.sunk | while | flops 59296340 | bytes 1905783 | solution.py:104
  219.3 5.7 %fusion.269 = (pred[64]{0:T(512)(128)(4,1)S(1)}, s32[64]{0:T(128)S(1)}, pred[64]{0:T(512)(128)(4,1)S(1)}) fusion(s32[64]{0:T(128)S(1)} %gather_fusion.7, s32[]{:T(128)} %bitcast.234, s32[]{:T(128)} %bitcast.235, s32[]{:T(128)} %bitcast.236, s32[]{:T(128)} %bitcast.237, s32[]{:T(128)} %bitcast.238, s32[]{:T(128)} %bitcast.239, s32[]{:T(128)} %bitcast.240, ...), kind=kLoop, calls=%fused_computation.202.clone.1 | loop fusion | flops 2048 | bytes 1196 | tf_op jit(solution)/shard_map/while/body/eq | solution.py:88
  228.8 16.9 %fusion.272 = f32[2,64,128]{2,0,1:T(2,128)S(1)} fusion(f32[64,128]{1,0:T(8,128)S(1)} %bitcast.297, f32[64,128]{1,0:T(8,128)S(1)} %bitcast.306, f32[64,128]{1,0:T(8,128)S(1)} %bitcast.304, f32[64,128]{1,0:T(8,128)S(1)} %broadcast_add_fusion.21, f32[64,128]{1,0:T(8,128)S(1)} %bitcast.305, f32[64,128]{1,0:T(8,128)S(1)} %broadcast_add_fusion.22, ...), kind=kOutput, calls=%fused_computation.164.clone.1 | convolution fusion | flops 57671680 | bytes 409728 | tf_op jit(solution)/shard_map/while/body/gij,kgj->kgi/dot_general | solution.py:98
  245.9 1.0 copy.40
  247.0 42.1 %reduce-scatter.12.cloned.1.call-done = f32[256,2]{1,0:T(8,128)} async-done(((f32[1024,2]{1,0:T(8,128)}), f32[256,2]{1,0:T(8,128)}) %reduce-scatter.12.cloned.1.call-update) | async-done | bytes 2064
  289.1 1.0 copy.36
  290.3 39.3 %all-reduce.3 = (f32[2]{0:T(128)S(1)}, f32[2]{0:T(128)S(1)}) all-reduce(f32[2]{0:T(128)S(1)} %get-tuple-element.1152, f32[2]{0:T(128)S(1)} %get-tuple-element.1151), channel_id=1, replica_groups=mesh['row'=4,'col'=8] {'row','col'}, use_global_device_ids=true, to_apply=%region_17.19 | all-reduce | flops 4 | bytes 32 | tf_op jit(solution)/shard_map/psum | solution.py:43
  329.7 26.1 %all_gather.19 = f32[2,2048]{1,0:T(2,128)S(1)} all-gather(f32[2,256]{1,0:T(2,128)S(1)} %multiply_subtract_fusion), channel_id=1, replica_groups=mesh['row'=4,'col'=8] {'col'}, dimensions={1}, use_global_device_ids=true | all-gather | bytes 18432 | tf_op jit(solution)/shard_map/all_gather | solution.py:94
  355.8 28.2 %while.50 = (s32[]{:T(128)}, f32[2,8,128]{2,1,0:T(8,128)S(1)}, s32[]{:T(128)}, s32[192]{0:T(256)S(1)}, f32[2,16,128]{2,0,1:T(2,128)S(1)}, /*index=5*/s32[]{:T(12...) while((s32[]{:T(128)}, f32[2,8,128]{2,1,0:T(8,128)S(1)}, ...), condition=%wide.region_26.28_spmd.clone.clone.clone, body=%wide.region_25.27_spmd.sunk.clone.clone.clone.sunk | while | flops 59296340 | bytes 1905783 | solution.py:104
  357.4 5.7 %fusion.280 = (pred[64]{0:T(512)(128)(4,1)S(1)}, s32[64]{0:T(128)S(1)}, pred[64]{0:T(512)(128)(4,1)S(1)}) fusion(s32[64]{0:T(128)S(1)} %gather_fusion.13, s32[]{:T(128)} %bitcast.257, s32[]{:T(128)} %bitcast.258, s32[]{:T(128)} %bitcast.259, s32[]{:T(128)} %bitcast.260, s32[]{:T(128)} %bitcast.261, s32[]{:T(128)} %bitcast.262, s32[]{:T(128)} %bitcast.263, ...), kind=kLoop, calls=%fused_computation.295.clone.1 | loop fusion | flops 2048 | bytes 1196 | tf_op jit(solution)/shard_map/while/body/eq | solution.py:88
  366.9 16.9 %fusion.283 = f32[2,64,128]{2,0,1:T(2,128)S(1)} fusion(f32[64,128]{1,0:T(8,128)S(1)} %bitcast.298, f32[64,128]{1,0:T(8,128)S(1)} %bitcast.310, f32[64,128]{1,0:T(8,128)S(1)} %bitcast.308, f32[64,128]{1,0:T(8,128)S(1)} %broadcast_add_fusion.24, f32[64,128]{1,0:T(8,128)S(1)} %bitcast.309, f32[64,128]{1,0:T(8,128)S(1)} %broadcast_add_fusion.25, ...), kind=kOutput, calls=%fused_computation.257.clone.1 | convolution fusion | flops 57671680 | bytes 409728 | tf_op jit(solution)/shard_map/while/body/gij,kgj->kgi/dot_general | solution.py:98
  384.0 1.0 copy.41
  385.1 42.1 %reduce-scatter.14.cloned.1.call-done = f32[256,2]{1,0:T(8,128)} async-done(((f32[1024,2]{1,0:T(8,128)}), f32[256,2]{1,0:T(8,128)}) %reduce-scatter.14.cloned.1.call-update) | async-done | bytes 2064
  427.2 1.0 copy.38
  428.3 39.3 %all-reduce.2 = (f32[2]{0:T(128)S(1)}, f32[2]{0:T(128)S(1)}) all-reduce(f32[2]{0:T(128)S(1)} %get-tuple-element.1150, f32[2]{0:T(128)S(1)} %get-tuple-element.1149), channel_id=1, replica_groups=mesh['row'=4,'col'=8] {'row','col'}, use_global_device_ids=true, to_apply=%region_24.26 | all-reduce | flops 4 | bytes 32 | tf_op jit(solution)/shard_map/psum | solution.py:43
  467.8 21.1 %psum.62 = f32[2]{0:T(128)S(1)} all-reduce(f32[2]{0:T(128)S(1)} %get-tuple-element.1248), channel_id=1, replica_groups=mesh['row'=4,'col'=8] {'col'}, use_global_device_ids=true, to_apply=%region_31.33 | all-reduce | flops 2 | bytes 16 | tf_op jit(solution)/shard_map/psum | solution.py:13
  488.9 5.6 %psum.63 = f32[2]{0:T(128)S(1)} all-reduce(f32[2]{0:T(128)S(1)} %psum.62), channel_id=1, replica_groups=mesh['row'=4,'col'=8] {'row'}, use_global_device_ids=true, to_apply=%region_32.34 | all-reduce | flops 2 | bytes 16 | tf_op jit(solution)/shard_map/psum | solution.py:13
  (111 shorter events, 22.6 us)
Async XLA Ops:
  6.5 144.5 %reduce-scatter.10.cloned.1.call-start = ((), (), s32[]{:S(2)}) async-start(), calls=%async_computation.3 | async-start | bytes 655360
  108.4 180.7 %reduce-scatter.12.cloned.1.call-start = ((), (), s32[]{:S(2)}) async-start(), calls=%async_computation.4 | async-start | bytes 655360
  247.0 180.2 %reduce-scatter.14.cloned.1.call-start = ((), (), s32[]{:S(2)}) async-start(), calls=%async_computation.5 | async-start | bytes 655360
Sparse Core Ops, SparseCore 0:
  108.6 42.4 reduce-scatter.9
  247.1 41.9 reduce-scatter.11
  385.2 41.9 reduce-scatter.13
